TPU v7x, 256 devices: a whole 4x4x8 slice. The times are simulated.
256 devices in a mesh: dp: 2 (over x_lo), fsdp: 16 (over x_hi, y, core), tensor: 8 (over z).
Axes of the slice: x: 4 (x_hi: 2, x_lo: 2; x = x_hi * 2 + x_lo), y: 4, z: 8, core: 2. Of those that a mesh axis runs over, the one named last changes fastest.
Arguments:
- hidden: bfloat16 [16384, 2048], P(('dp', 'fsdp'), 'tensor'), may hold values from -8 to 8
- norm_gain: bfloat16 [2048], P('tensor'), may hold values from 0.099609375 to 1.8984375
- head_weight: bfloat16 [2048, 32128], P('fsdp', 'tensor'), may hold values from -1 to 1
- token_ids: int32 [32, 512], P(('dp', 'fsdp')), may hold values from 0 to 32127
- lengths: int32 [32], P(('dp', 'fsdp')), may hold values from 128 to 512
- old_logp: float32 [32, 512], P(('dp', 'fsdp')), may hold values from -12.5 to -9.5
- advantages: float32 [32, 512], P(('dp', 'fsdp')), may hold values from -4 to 4
- rollout_logp: float32 [32, 512], P(('dp', 'fsdp'), 'tensor'), may hold values from -16 to -1
- rollout_row: int32 [32], P(('dp', 'fsdp')), may hold values from 0 to 31, each once
Outputs:
- new_logp: float32 [32, 512], P(('dp', 'fsdp'))
- token_loss: float32 [32, 512], P(('dp', 'fsdp'))
- summary: float32 [3], replicated
Inputs may be any that keep to these rules, and one draw needn't show every extreme that they name: `rollout_row`: every row 0 to 31 is named once.
All inputs are finite; a program needn't handle non-finite values.
Results may differ from a plain program's by a relative error of at most 0.0005.
The roundings to bfloat16 on the way count: a program that leaves them out, or rounds other values in their place, can miss the bound.
Values may be sent and summed in bfloat16 or wider, within the bound.
A program may use at most 128 MiB of HBM per device.

v0:
```python
import jax
import jax.numpy as jnp
from jax import lax
from jax.sharding import PartitionSpec as P

clip_eps = 0.2
kl_coef = 0.2
log_limit = 10.0
norm_eps = 1e-06


def copy_for_each(array, axis):
    copies = jnp.broadcast_to(array, (lax.axis_size(axis), *array.shape))
    return lax.all_to_all(copies, axis, split_axis=0, concat_axis=0, tiled=True)


def taken_together(array, axis):
    everything = copy_for_each(array, axis)
    return jnp.max(everything, axis=0)


def taken_together_2(array, axis):
    everything = copy_for_each(array, axis)
    return jnp.sum(everything, axis=0)


def in_one(arrays, axis):
    line, at, outs = (jnp.concatenate([a.reshape(-1) for a in arrays]), 0, [])
    so_far = taken_together_2(line, axis)
    for a in arrays:
        outs.append(so_far[at : at + a.size].reshape(a.shape))
        at += a.size
    return tuple(outs)


def joined_along(tiles, dim):
    lengths = list(tiles.shape[1:])
    lengths[dim] *= tiles.shape[0]
    return jnp.moveaxis(tiles, 0, dim).reshape(lengths)


def collect(array, axis, dim):
    return joined_along(copy_for_each(array, axis), dim)


def token_terms(new_logp, old_logp, advantages, ref_logp, live_mask, prob_square):
    shift = new_logp - old_logp
    prob_ratio = jnp.exp(jnp.clip(shift, -log_limit, log_limit))
    clipped = jnp.clip(prob_ratio, 1.0 - clip_eps, 1.0 + clip_eps)
    plain_term = prob_ratio * advantages
    bounded_term = clipped * advantages
    surrogate = jnp.minimum(plain_term, bounded_term)
    ref_gap = ref_logp - new_logp
    gap_clip = jnp.clip(ref_gap, -log_limit, log_limit)
    kl_term = jnp.exp(gap_clip) - gap_clip - 1.0
    token_loss = live_mask * (kl_coef * kl_term - surrogate)
    inside_gap = (jnp.abs(ref_gap) < log_limit).astype(jnp.float32)
    inside_ratio = (jnp.abs(shift) < log_limit).astype(jnp.float32)
    active_term = (plain_term <= bounded_term).astype(jnp.float32)
    grad_coef = live_mask * (
        kl_coef * (1.0 - jnp.exp(gap_clip)) * inside_gap
        - advantages * prob_ratio * active_term * inside_ratio
    )
    grad_square = grad_coef * grad_coef * (prob_square - 2.0 * jnp.exp(new_logp) + 1.0)
    return (token_loss, live_mask * kl_term, grad_square)


def exp_sums(logits, row_max):
    shifted = jnp.exp(logits - row_max[:, None])
    return (jnp.sum(shifted, axis=1), jnp.sum(shifted * shifted, axis=1))


def vocab_stats(logits, flat_ids, col_start):
    col_ids = lax.broadcasted_iota(jnp.int32, logits.shape, 1) + col_start
    picked = jnp.sum(jnp.where(col_ids == flat_ids[:, None], logits, 0.0), axis=1)
    local_max = jnp.max(logits, axis=1)
    row_max = taken_together(local_max, "tensor")
    exp_sum, exp_square = exp_sums(logits, row_max)
    exp_sum, exp_square, picked = in_one((exp_sum, exp_square, picked), "tensor")
    return (row_max, exp_sum, exp_square, picked)


def shards(
    hidden,
    norm_gain,
    head_weight,
    token_ids,
    lengths,
    old_logp,
    advantages,
    rollout_logp,
    rollout_row,
):
    full_rows, full_gain = (collect(hidden, "tensor", 1), collect(norm_gain, "tensor", 0))
    values = full_rows.astype(jnp.float32)
    inv_rms = lax.rsqrt(jnp.mean(values * values, axis=1, keepdims=True) + norm_eps)
    normed = (values * inv_rms * full_gain.astype(jnp.float32)[None, :]).astype(jnp.bfloat16)
    flat_ids = token_ids.reshape(-1)
    vocab_cols = head_weight.shape[1]
    tensor_pos = lax.axis_index("tensor")
    logits = jnp.dot(
        normed,
        lax.all_gather(head_weight, "fsdp", axis=0, tiled=True),
        preferred_element_type=jnp.float32,
    )
    soft_stats = vocab_stats(logits, flat_ids, tensor_pos * vocab_cols)
    row_max, exp_sum, exp_square, picked = soft_stats
    new_logp = (picked - row_max - jnp.log(exp_sum)).reshape(token_ids.shape)
    prob_square = (exp_square / (exp_sum * exp_sum)).reshape(token_ids.shape)
    ref_all = collect(rollout_logp, ("dp", "fsdp"), 0)
    own_ref = jnp.take(ref_all, rollout_row, axis=0)
    ref_logp = collect(own_ref, "tensor", 1)
    positions = lax.broadcasted_iota(jnp.int32, token_ids.shape, 1)
    live_mask = (positions < lengths[:, None]).astype(jnp.float32)
    token_loss, kl_part, grad_part = token_terms(
        new_logp, old_logp, advantages, ref_logp, live_mask, prob_square
    )
    live_count, loss_sum, kl_sum, grad_sum = in_one(
        (jnp.sum(live_mask), jnp.sum(token_loss), jnp.sum(kl_part), jnp.sum(grad_part)),
        ("dp", "fsdp"),
    )
    summary = jnp.stack(
        [loss_sum / live_count, kl_sum / live_count, jnp.sqrt(grad_sum / live_count)]
    )
    return (new_logp, token_loss, summary)


def solution(mesh):
    in_specs = (
        P(("dp", "fsdp"), "tensor"),
        P("tensor"),
        P("fsdp", "tensor"),
        P(("dp", "fsdp"), None),
        P(("dp", "fsdp")),
        P(("dp", "fsdp"), None),
        P(("dp", "fsdp"), None),
        P(("dp", "fsdp"), "tensor"),
        P(("dp", "fsdp")),
    )
    out_specs = (P(("dp", "fsdp"), None), P(("dp", "fsdp"), None), P())
    return jax.shard_map(shards, mesh=mesh, in_specs=in_specs, out_specs=out_specs, check_vma=False)
```

profile of v0, /device:TPU:1, one launch (start us, length us, event | category | flops | bytes accessed | tf_op | source)
XLA Modules:
  0.0 218.8 jit_solution(17460148132570036709)
XLA Ops:
  7.2 0.7 all-gather.2.cloned.1.call-update
  7.9 0.7 broadcast_in_dim.42
  9.1 0.7 reduce.12
  9.8 0.6 reshape.211
  10.4 9.0 %all-to-all-start.1 = ((bf16[8,2,128]{2,1,0:T(2,128)(2,1)}), bf16[8,2,128]{2,1,0:T(2,128)(2,1)S(1)}, u32[]{:S(2)}, u32[]{:S(2)}) async-start(bf16[8,2,128]{2,1,0:T(2,128)(2,1)} %reshape.211), calls=%async_computation.1 | async-start | bytes 8192 | tf_op jit(solution)/shard_map/all_to_all | solution.py:14
  19.4 1.1 copy.14
  20.5 5.5 %all-to-all-done.1 = bf16[8,2,128]{2,1,0:T(2,128)(2,1)S(1)} async-done(((bf16[8,2,128]{2,1,0:T(2,128)(2,1)}), bf16[8,2,128]{2,1,0:T(2,128)(2,1)S(1)}, u32[]{:S(2)}, u32[]{:S(2)}) %all-to-all-start.1) | async-done | bytes 4128 | tf_op jit(solution)/shard_map/all_to_all | solution.py:14
  25.9 1.5 broadcast_in_dim.41
  27.4 3.6 %all-to-all-start = ((bf16[8,512,256]{1,2,0:T(8,128)(2,1)}), bf16[8,512,256]{1,2,0:T(8,128)(2,1)S(1)}, u32[]{:S(2)}, u32[]{:S(2)}) async-start(bf16[8,512,256]{1,2,0:T(8,128)(2,1)} %broadcast_in_dim.41), calls=%async_computation | async-start | bytes 4194304 | tf_op jit(solution)/shard_map/all_to_all | solution.py:14
  31.8 50.9 %all-to-all-done = bf16[8,512,256]{1,2,0:T(8,128)(2,1)S(1)} async-done(((bf16[8,512,256]{1,2,0:T(8,128)(2,1)}), bf16[8,512,256]{1,2,0:T(8,128)(2,1)S(1)}, u32[]{:S(2)}, u32[]{:S(2)}) %all-to-all-start) | async-done | bytes 2097184 | tf_op jit(solution)/shard_map/all_to_all | solution.py:14
  82.6 0.6 broadcast_in_dim.48
  83.2 7.6 %all-to-all-start.4 = ((f32[32,1,64]{2,1,0:T(1,128)}), f32[32,1,64]{2,1,0:T(1,128)S(1)}, u32[]{:S(2)}, u32[]{:S(2)}) async-start(f32[32,1,64]{2,1,0:T(1,128)} %broadcast_in_dim.48), calls=%async_computation.4 | async-start | bytes 32768 | tf_op jit(solution)/shard_map/all_to_all | solution.py:14
  91.4 2.0 fusion.2
  93.4 43.2 %all-gather.2.cloned.1.call-done = bf16[2048,4016]{0,1:T(8,128)(2,1)} async-done(((bf16[128,4016]{0,1:T(8,128)(2,1)}), bf16[2048,4016]{0,1:T(8,128)(2,1)}) %all-gather.2.cloned.1.call-update) | async-done | bytes 16449552 | tf_op jit(solution)/shard_map/all_gather | solution.py:103
  136.5 14.8 %fusion.18 = (f32[512]{0:T(512)S(1)}, f32[512,4016]{0,1:T(8,128)}) fusion(bf16[2048,4016]{0,1:T(8,128)(2,1)} %all-gather.2.cloned.1.call-done, bf16[512,2048]{0,1:T(8,128)(2,1)} %fusion.2), kind=kOutput, calls=%fused_computation.43 | convolution fusion | flops 8424218112 | bytes 26773504 | tf_op jit(solution)/shard_map/dot_general | solution.py:101
  151.3 0.6 broadcast_in_dim.43
  151.9 6.7 %all-to-all-start.2 = ((f32[8,1,512]{2,1,0:T(1,128)}), f32[8,1,512]{2,1,0:T(1,128)S(1)}, u32[]{:S(2)}, u32[]{:S(2)}) async-start(f32[8,1,512]{2,1,0:T(1,128)} %broadcast_in_dim.43), calls=%async_computation.2 | async-start | bytes 32768 | tf_op jit(solution)/shard_map/all_to_all | solution.py:14
  158.7 6.6 %all-to-all-done.2 = f32[8,1,512]{2,1,0:T(1,128)S(1)} async-done(((f32[8,1,512]{2,1,0:T(1,128)}), f32[8,1,512]{2,1,0:T(1,128)S(1)}, u32[]{:S(2)}, u32[]{:S(2)}) %all-to-all-start.2) | async-done | bytes 16416 | tf_op jit(solution)/shard_map/all_to_all | solution.py:14
  165.3 0.6 broadcast_in_dim.50
  165.9 3.3 %all-to-all-start.5 = ((f32[8,1,64]{2,1,0:T(1,128)}), f32[8,1,64]{2,1,0:T(1,128)S(1)}, u32[]{:S(2)}, u32[]{:S(2)}) async-start(f32[8,1,64]{2,1,0:T(1,128)} %broadcast_in_dim.50), calls=%async_computation.5 | async-start | bytes 8192 | tf_op jit(solution)/shard_map/all_to_all | solution.py:14
  169.3 5.4 %fusion = (f32[512]{0:T(512)S(1)}, f32[512]{0:T(512)S(1)}, f32[512]{0:T(512)S(1)}) fusion(f32[512,4016]{0,1:T(8,128)} %get-tuple-element.29, f32[512]{0:T(512)S(1)} %reduce_max.19, s32[512]{0:T(512)S(1)} %bitcast.36, s32[4016]{0:T(1024)S(1)} %iota_add_fusion), kind=kLoop, calls=%fused_computation.3 | loop fusion | flops 14391808 | bytes 8251072 | tf_op jit(solution)/shard_map/reduce_sum | solution.py:70
  174.7 1.0 all-to-all-done.5
  175.7 0.6 broadcast_in_dim.45
  176.3 5.6 %all-to-all-start.3 = ((f32[8,1,1536]{2,1,0:T(1,128)}), f32[8,1,1536]{2,1,0:T(1,128)S(1)}, u32[]{:S(2)}, u32[]{:S(2)}) async-start(f32[8,1,1536]{2,1,0:T(1,128)} %broadcast_in_dim.45), calls=%async_computation.3 | async-start | bytes 98304 | tf_op jit(solution)/shard_map/all_to_all | solution.py:14
  183.1 0.7 reduce.11
  183.9 5.1 %all-to-all-done.3 = f32[8,1,1536]{2,1,0:T(1,128)S(1)} async-done(((f32[8,1,1536]{2,1,0:T(1,128)}), f32[8,1,1536]{2,1,0:T(1,128)S(1)}, u32[]{:S(2)}, u32[]{:S(2)}) %all-to-all-start.3) | async-done | bytes 49184 | tf_op jit(solution)/shard_map/all_to_all | solution.py:14
  189.2 0.6 reduce_sum.97
  189.8 1.3 fusion.15
  191.1 2.6 %pad_maximum_fusion.1 = f32[4]{0:T(128)S(1)} fusion(f32[1]{0:T(128)} %bitcast.17, f32[1]{0:T(128)} %bitcast.14, f32[1]{0:T(128)} %bitcast.12, f32[1]{0:T(128)} %bitcast.11), kind=kLoop, calls=%fused_computation.38 | loop fusion | flops 12 | bytes 32 | tf_op jit(solution)/shard_map/concatenate | solution.py:28
  193.7 13.1 %all_to_all.39 = f32[32,1,4]{2,1,0:T(1,128)S(1)} all-to-all(f32[32,1,4]{2,1,0:T(1,128)S(1)} %broadcast_in_dim.51), channel_id=1, replica_groups=mesh['dp'=2,'fsdp'=16,'tensor'=8] {'dp','fsdp'}, dimensions={0} | all-to-all | bytes 1024 | tf_op jit(solution)/shard_map/all_to_all | solution.py:14
  206.9 0.7 fusion.17
  211.3 0.6 pad_maximum_fusion.2
  (30 shorter events, 2.0 us)
Async XLA Ops:
  7.2 75.5 %copy-start.4 = (f32[1,64]{1,0:T(1,128)S(1)}, f32[1,64]{1,0:T(1,128)}, u32[]{:S(2)}) copy-start(f32[1,64]{1,0:T(1,128)} %param.16) | copy-start | bytes 772
  7.2 129.3 %all-gather.2.cloned.1.call-start = ((), (), s32[]{:S(2)}) async-start(), calls=%async_computation.7 | async-start | bytes 17477632 | tf_op jit(solution)/shard_map/all_gather | solution.py:103
  10.4 15.6 %all-to-all-start.1 = ((bf16[8,2,128]{2,1,0:T(2,128)(2,1)}), bf16[8,2,128]{2,1,0:T(2,128)(2,1)S(1)}, u32[]{:S(2)}, u32[]{:S(2)}) async-start(bf16[8,2,128]{2,1,0:T(2,128)(2,1)} %reshape.211), calls=%async_computation.1 | async-start | bytes 8192 | tf_op jit(solution)/shard_map/all_to_all | solution.py:14
  27.4 55.2 %all-to-all-start = ((bf16[8,512,256]{1,2,0:T(8,128)(2,1)}), bf16[8,512,256]{1,2,0:T(8,128)(2,1)S(1)}, u32[]{:S(2)}, u32[]{:S(2)}) async-start(bf16[8,512,256]{1,2,0:T(8,128)(2,1)} %broadcast_in_dim.41), calls=%async_computation | async-start | bytes 4194304 | tf_op jit(solution)/shard_map/all_to_all | solution.py:14
  83.2 68.1 %all-to-all-start.4 = ((f32[32,1,64]{2,1,0:T(1,128)}), f32[32,1,64]{2,1,0:T(1,128)S(1)}, u32[]{:S(2)}, u32[]{:S(2)}) async-start(f32[32,1,64]{2,1,0:T(1,128)} %broadcast_in_dim.48), calls=%async_computation.4 | async-start | bytes 32768 | tf_op jit(solution)/shard_map/all_to_all | solution.py:14
  93.4 75.9 %copy-start.3 = (s32[1,512]{1,0:T(1,128)S(1)}, s32[1,512]{1,0:T(1,128)}, u32[]{:S(2)}) copy-start(s32[1,512]{1,0:T(1,128)} %param.12) | copy-start | bytes 6148
  151.9 13.4 %all-to-all-start.2 = ((f32[8,1,512]{2,1,0:T(1,128)}), f32[8,1,512]{2,1,0:T(1,128)S(1)}, u32[]{:S(2)}, u32[]{:S(2)}) async-start(f32[8,1,512]{2,1,0:T(1,128)} %broadcast_in_dim.43), calls=%async_computation.2 | async-start | bytes 32768 | tf_op jit(solution)/shard_map/all_to_all | solution.py:14
  165.9 9.8 %all-to-all-start.5 = ((f32[8,1,64]{2,1,0:T(1,128)}), f32[8,1,64]{2,1,0:T(1,128)S(1)}, u32[]{:S(2)}, u32[]{:S(2)}) async-start(f32[8,1,64]{2,1,0:T(1,128)} %broadcast_in_dim.50), calls=%async_computation.5 | async-start | bytes 8192 | tf_op jit(solution)/shard_map/all_to_all | solution.py:14
  169.3 20.6 %copy-start.1 = (f32[1,512]{1,0:T(1,128)S(1)}, f32[1,512]{1,0:T(1,128)}, u32[]{:S(2)}) copy-start(f32[1,512]{1,0:T(1,128)} %param.15) | copy-start | bytes 6148
  169.3 20.6 %copy-start.2 = (f32[1,512]{1,0:T(1,128)S(1)}, f32[1,512]{1,0:T(1,128)}, u32[]{:S(2)}) copy-start(f32[1,512]{1,0:T(1,128)} %param.14) | copy-start | bytes 6148
  176.3 12.7 %all-to-all-start.3 = ((f32[8,1,1536]{2,1,0:T(1,128)}), f32[8,1,1536]{2,1,0:T(1,128)S(1)}, u32[]{:S(2)}, u32[]{:S(2)}) async-start(f32[8,1,1536]{2,1,0:T(1,128)} %broadcast_in_dim.45), calls=%async_computation.3 | async-start | bytes 98304 | tf_op jit(solution)/shard_map/all_to_all | solution.py:14
  189.1 22.9 %copy-start = (f32[512]{0:T(512)}, f32[512]{0:T(512)S(1)}, u32[]{:S(2)}) copy-start(f32[512]{0:T(512)S(1)} %get-tuple-element.20) | copy-start | bytes 6148
Sparse Core Ops, SparseCore 0:
  10.5 125.9 all-gather.1
where the time goes:
time: 219 us
  waiting for transfers between devices  113 us (52%)
  starting transfers between devices  36 us (16%)
  between operations  19.3 us (9%)
  matrix products  14.8 us (7%)
  other arithmetic  14.5 us (7%)
  blocking collectives  13.1 us (6%)
  local copies, waits for them, and re-layouts  8.21 us (4%)
    all_to_all x6, waiting for transfers between devices, copy_for_each(): return lax.all_to_all(copies, axis, split_axis=0, concat_axis=0, tiled=True)  69 us
    all_gather x1, waiting for transfers between devices, shards(): lax.all_gather(head_weight, 'fsdp', axis=0, tiled=True)  43.2 us
    all_to_all x6, starting transfers between devices, copy_for_each(): return lax.all_to_all(copies, axis, split_axis=0, concat_axis=0, tiled=True)  35.9 us
    dot_general x1, matrix products, shards(): jnp.dot(normed, lax.all_gather(head_weight, 'fsdp', axis=0, tiled=True),...  14.8 us
    all_to_all x1, blocking collectives, copy_for_each(): return lax.all_to_all(copies, axis, split_axis=0, concat_axis=0, tiled=True)  13.1 us
    reduce_sum x1, other arithmetic, exp_sums(): return (jnp.sum(shifted, axis=1), jnp.sum(shifted * shifted, axis=1))  5.43 us
    broadcast_in_dim x8, local copies, waits for them, and re-layouts, copy_for_each(): copies = jnp.broadcast_to(array, (lax.axis_size(axis), *array.shape))  5.14 us
  transfers between devices with their start and end apart: 7, of which 6 were waited for; matrix products, arithmetic and copies ran while one was open for 14% of the time, Pallas kernels for 0%

commit v1 on v0

--- a/solution.py
+++ b/solution.py
@@ -98,11 +98,15 @@
     flat_ids = token_ids.reshape(-1)
     vocab_cols = head_weight.shape[1]
     tensor_pos = lax.axis_index("tensor")
-    logits = jnp.dot(
-        normed,
-        lax.all_gather(head_weight, "fsdp", axis=0, tiled=True),
-        preferred_element_type=jnp.float32,
-    )
+
+    def turn_shelves(row_data, mesh_ax):
+        local_now = lax.axis_size(mesh_ax)
+        tall = jnp.stack(local_now * [row_data], 0)
+        low = lax.all_to_all(tall, mesh_ax, 0, 0)
+        fresh = jnp.concatenate(low, 0)
+        return fresh
+
+    logits = jnp.dot(normed, turn_shelves(head_weight, "fsdp"), preferred_element_type=jnp.float32)
     soft_stats = vocab_stats(logits, flat_ids, tensor_pos * vocab_cols)
     row_max, exp_sum, exp_square, picked = soft_stats
     new_logp = (picked - row_max - jnp.log(exp_sum)).reshape(token_ids.shape)

time: 219 us -> 449 us (2.05)
  waiting for transfers between devices: 113 us -> 264 us
  blocking collectives: 13.1 us -> 67.8 us
  local copies, waits for them, and re-layouts: 8.21 us -> 34.6 us
  between operations: 19.3 us -> 5.9 us
  starting transfers between devices: 36 us -> 45.9 us
    all_to_all x0 -> x1, waiting for transfers between devices: none -> 246 us  [turn_shelves(): low = lax.all_to_all(tall, mesh_ax, 0, 0)]
    all_to_all x1 -> x2, blocking collectives: 13.1 us -> 67.8 us  [copy_for_each(): return lax.all_to_all(copies, axis, split_axis=0, concat_axis=0, tiled=True)]
    all_to_all x6 -> x5, waiting for transfers between devices: 69 us -> 18.1 us  [copy_for_each(): return lax.all_to_all(copies, axis, split_axis=0, concat_axis=0, tiled=True)]
    all_gather x1 -> x0, waiting for transfers between devices: 43.2 us -> none  [shards(): lax.all_gather(head_weight, 'fsdp', axis=0, tiled=True)]
    all_to_all x0 -> x1, local copies, waits for them, and re-layouts: none -> 20.9 us  [turn_shelves(): low = lax.all_to_all(tall, mesh_ax, 0, 0)]
    all_to_all x0 -> x1, starting transfers between devices: none -> 10.9 us  [turn_shelves(): low = lax.all_to_all(tall, mesh_ax, 0, 0)]
    another operation x0 -> x1, local copies, waits for them, and re-layouts: none -> 6.85 us  [turn_shelves(): tall = jnp.stack(local_now * [row_data], 0)]
    all_to_all x6 -> x5, starting transfers between devices: 35.9 us -> 35 us  [copy_for_each(): return lax.all_to_all(copies, axis, split_axis=0, concat_axis=0, tiled=True)]
  transfers between devices with their start and end apart: 7 -> 6, of which waited for: 6 -> 5; matrix products, arithmetic and copies ran while one was open for 14% -> 10% of each run, Pallas kernels for 0% -> 0%
where the time goes in v1:
time: 449 us; the launch traced here: 448 us
  waiting for transfers between devices  264 us (59%)
  blocking collectives  67.8 us (15%)
  starting transfers between devices  45.9 us (10%)
  local copies, waits for them, and re-layouts  34.6 us (8%)
  other arithmetic  14.5 us (3%)
  matrix products  14.4 us (3%)
  between operations  5.9 us (1%)
    all_to_all x1, waiting for transfers between devices, turn_shelves(): low = lax.all_to_all(tall, mesh_ax, 0, 0)  246 us
    all_to_all x2, blocking collectives, copy_for_each(): return lax.all_to_all(copies, axis, split_axis=0, concat_axis=0, tiled=True)  67.8 us
    all_to_all x5, starting transfers between devices, copy_for_each(): return lax.all_to_all(copies, axis, split_axis=0, concat_axis=0, tiled=True)  35 us
    all_to_all x1, local copies, waits for them, and re-layouts, turn_shelves(): low = lax.all_to_all(tall, mesh_ax, 0, 0)  20.9 us
    all_to_all x5, waiting for transfers between devices, copy_for_each(): return lax.all_to_all(copies, axis, split_axis=0, concat_axis=0, tiled=True)  18.1 us
    dot_general x1, matrix products, shards(): jnp.dot(normed, turn_shelves(head_weight, 'fsdp'), preferred_element_type...  14.4 us
    all_to_all x1, starting transfers between devices, turn_shelves(): low = lax.all_to_all(tall, mesh_ax, 0, 0)  10.9 us
  transfers between devices with their start and end apart: 6, of which 5 were waited for; matrix products, arithmetic and copies ran while one was open for 10% of the time, Pallas kernels for 0%

profile of v1, /device:TPU:1, one launch (start us, length us, event | category | flops | bytes accessed | tf_op | source)
XLA Modules:
  0.0 447.5 jit_solution(17906040013475217199)
XLA Ops:
  0.6 0.7 broadcast_in_dim.42
  1.8 0.7 reduce.12
  2.5 0.6 reshape.225
  3.1 9.0 %all-to-all-start.1 = ((bf16[8,2,128]{2,1,0:T(2,128)(2,1)}), bf16[8,2,128]{2,1,0:T(2,128)(2,1)S(1)}, u32[]{:S(2)}, u32[]{:S(2)}) async-start(bf16[8,2,128]{2,1,0:T(2,128)(2,1)} %reshape.225), calls=%async_computation.1 | async-start | bytes 8192 | tf_op jit(solution)/shard_map/all_to_all | solution.py:14
  12.1 1.1 copy.20
  13.2 5.5 %all-to-all-done.1 = bf16[8,2,128]{2,1,0:T(2,128)(2,1)S(1)} async-done(((bf16[8,2,128]{2,1,0:T(2,128)(2,1)}), bf16[8,2,128]{2,1,0:T(2,128)(2,1)S(1)}, u32[]{:S(2)}, u32[]{:S(2)}) %all-to-all-start.1) | async-done | bytes 4128 | tf_op jit(solution)/shard_map/all_to_all | solution.py:14
  18.8 50.8 %all_to_all.44 = bf16[8,512,256]{1,2,0:T(8,128)(2,1)S(1)} all-to-all(bf16[8,512,256]{1,2,0:T(8,128)(2,1)S(1)} %broadcast_in_dim.41), channel_id=1, replica_groups=mesh['dp'=2,'fsdp'=16,'tensor'=8] {'tensor'}, dimensions={0} | all-to-all | bytes 4194304 | tf_op jit(solution)/shard_map/all_to_all | solution.py:14
  69.6 6.8 %stack.4 = bf16[16,128,4016]{1,2,0:T(8,128)(2,1)} broadcast(bf16[128,4016]{0,1:T(8,128)(2,1)} %param.11), dimensions={1,2} | broadcast | bytes 17477632 | tf_op jit(solution)/shard_map/stack | solution.py:104
  76.5 10.9 %all-to-all-start.2 = ((bf16[16,128,4016]{1,2,0:T(8,128)(2,1)}), bf16[16,128,4016]{1,2,0:T(8,128)(2,1)}, u32[]{:S(2)}, u32[]{:S(2)}) async-start(bf16[16,128,4016]{1,2,0:T(8,128)(2,1)} %stack.4), calls=%async_computation.2 | async-start | bytes 32899072 | tf_op jit(solution)/shard_map/all_to_all | solution.py:105
  88.6 1.9 fusion.3
  90.4 246.3 %all-to-all-done.2 = bf16[16,128,4016]{1,2,0:T(8,128)(2,1)} async-done(((bf16[16,128,4016]{1,2,0:T(8,128)(2,1)}), bf16[16,128,4016]{1,2,0:T(8,128)(2,1)}, u32[]{:S(2)}, u32[]{:S(2)}) %all-to-all-start.2) | async-done | bytes 16449568 | tf_op jit(solution)/shard_map/all_to_all | solution.py:105
  336.7 0.6 broadcast_in_dim.48
  337.3 13.8 %all-to-all-start.5 = ((f32[32,1,64]{2,1,0:T(1,128)}), f32[32,1,64]{2,1,0:T(1,128)S(1)}, u32[]{:S(2)}, u32[]{:S(2)}) async-start(f32[32,1,64]{2,1,0:T(1,128)} %broadcast_in_dim.48), calls=%async_computation.5 | async-start | bytes 32768 | tf_op jit(solution)/shard_map/all_to_all | solution.py:14
  351.1 20.9 %copy.21 = bf16[16,128,4016]{2,1,0:T(8,128)(2,1)} copy(bf16[16,128,4016]{1,2,0:T(8,128)(2,1)} %all-to-all-done.2) | data formatting | bytes 32899072 | tf_op jit(solution)/shard_map/all_to_all | solution.py:105
  372.0 14.4 %fusion.19 = (f32[512]{0:T(512)S(1)}, f32[512,4016]{0,1:T(8,128)}) fusion(bf16[512,2048]{0,1:T(8,128)(2,1)S(1)} %bitcast.28, bf16[2048,4016]{1,0:T(8,128)(2,1)} %bitcast.27), kind=kOutput, calls=%fused_computation.45 | convolution fusion | flops 8424218112 | bytes 26773504 | tf_op jit(solution)/shard_map/dot_general | solution.py:109
  386.4 0.6 broadcast_in_dim.43
  387.0 3.3 all-to-all-start.3
  390.4 6.5 %all-to-all-done.3 = f32[8,1,512]{2,1,0:T(1,128)S(1)} async-done(((f32[8,1,512]{2,1,0:T(1,128)}), f32[8,1,512]{2,1,0:T(1,128)S(1)}, u32[]{:S(2)}, u32[]{:S(2)}) %all-to-all-start.3) | async-done | bytes 16416 | tf_op jit(solution)/shard_map/all_to_all | solution.py:14
  396.9 0.6 broadcast_in_dim.50
  397.5 3.3 all-to-all-start.6
  400.9 5.5 %fusion = (f32[512]{0:T(512)S(1)}, f32[512]{0:T(512)S(1)}, f32[512]{0:T(512)S(1)}) fusion(f32[512,4016]{0,1:T(8,128)} %get-tuple-element.29, f32[512]{0:T(512)S(1)} %reduce_max.19, s32[512]{0:T(512)S(1)} %bitcast.36, s32[4016]{0:T(1024)S(1)} %iota_add_fusion), kind=kLoop, calls=%fused_computation.3 | loop fusion | flops 14391808 | bytes 8251072 | tf_op jit(solution)/shard_map/reduce_sum | solution.py:70
  406.4 1.0 all-to-all-done.6
  407.3 0.6 broadcast_in_dim.45
  408.0 5.6 %all-to-all-start.4 = ((f32[8,1,1536]{2,1,0:T(1,128)}), f32[8,1,1536]{2,1,0:T(1,128)S(1)}, u32[]{:S(2)}, u32[]{:S(2)}) async-start(f32[8,1,1536]{2,1,0:T(1,128)} %broadcast_in_dim.45), calls=%async_computation.4 | async-start | bytes 98304 | tf_op jit(solution)/shard_map/all_to_all | solution.py:14
  414.8 0.7 reduce.11
  415.5 5.1 %all-to-all-done.4 = f32[8,1,1536]{2,1,0:T(1,128)S(1)} async-done(((f32[8,1,1536]{2,1,0:T(1,128)}), f32[8,1,1536]{2,1,0:T(1,128)S(1)}, u32[]{:S(2)}, u32[]{:S(2)}) %all-to-all-start.4) | async-done | bytes 49184 | tf_op jit(solution)/shard_map/all_to_all | solution.py:14
  420.8 0.6 reduce_sum.97
  421.5 1.3 fusion.16
  422.8 2.6 pad_maximum_fusion.1
  425.4 17.0 %all_to_all.45 = f32[32,1,4]{2,1,0:T(1,128)S(1)} all-to-all(f32[32,1,4]{2,1,0:T(1,128)S(1)} %broadcast_in_dim.51), channel_id=1, replica_groups=mesh['dp'=2,'fsdp'=16,'tensor'=8] {'dp','fsdp'}, dimensions={0} | all-to-all | bytes 1024 | tf_op jit(solution)/shard_map/all_to_all | solution.py:14
  442.4 0.7 fusion.18
  446.9 0.6 pad_maximum_fusion.2
  (32 shorter events, 2.1 us)
Async XLA Ops:
  3.1 15.6 %all-to-all-start.1 = ((bf16[8,2,128]{2,1,0:T(2,128)(2,1)}), bf16[8,2,128]{2,1,0:T(2,128)(2,1)S(1)}, u32[]{:S(2)}, u32[]{:S(2)}) async-start(bf16[8,2,128]{2,1,0:T(2,128)(2,1)} %reshape.225), calls=%async_computation.1 | async-start | bytes 8192 | tf_op jit(solution)/shard_map/all_to_all | solution.py:14
  76.5 260.3 %copy-start.5 = (f32[1,64]{1,0:T(1,128)S(1)}, f32[1,64]{1,0:T(1,128)}, u32[]{:S(2)}) copy-start(f32[1,64]{1,0:T(1,128)} %param.16) | copy-start | bytes 772
  76.5 260.3 %all-to-all-start.2 = ((bf16[16,128,4016]{1,2,0:T(8,128)(2,1)}), bf16[16,128,4016]{1,2,0:T(8,128)(2,1)}, u32[]{:S(2)}, u32[]{:S(2)}) async-start(bf16[16,128,4016]{1,2,0:T(8,128)(2,1)} %stack.4), calls=%async_computation.2 | async-start | bytes 32899072 | tf_op jit(solution)/shard_map/all_to_all | solution.py:105
  337.3 49.1 %all-to-all-start.5 = ((f32[32,1,64]{2,1,0:T(1,128)}), f32[32,1,64]{2,1,0:T(1,128)S(1)}, u32[]{:S(2)}, u32[]{:S(2)}) async-start(f32[32,1,64]{2,1,0:T(1,128)} %broadcast_in_dim.48), calls=%async_computation.5 | async-start | bytes 32768 | tf_op jit(solution)/shard_map/all_to_all | solution.py:14
  351.1 20.9 %copy-start = (bf16[8,512,256]{1,2,0:T(8,128)(2,1)S(1)}, bf16[8,512,256]{1,2,0:T(8,128)(2,1)}, u32[]{:S(2)}) copy-start(bf16[8,512,256]{1,2,0:T(8,128)(2,1)} %fusion.3) | copy-start | bytes 6291460
  372.0 28.9 %copy-start.4 = (s32[1,512]{1,0:T(1,128)S(1)}, s32[1,512]{1,0:T(1,128)}, u32[]{:S(2)}) copy-start(s32[1,512]{1,0:T(1,128)} %param.12) | copy-start | bytes 6148
  386.4 35.1 %copy-start.2 = (f32[1,512]{1,0:T(1,128)S(1)}, f32[1,512]{1,0:T(1,128)}, u32[]{:S(2)}) copy-start(f32[1,512]{1,0:T(1,128)} %param.15) | copy-start | bytes 6148
  386.4 35.1 %copy-start.3 = (f32[1,512]{1,0:T(1,128)S(1)}, f32[1,512]{1,0:T(1,128)}, u32[]{:S(2)}) copy-start(f32[1,512]{1,0:T(1,128)} %param.14) | copy-start | bytes 6148
  387.0 9.9 %all-to-all-start.3 = ((f32[8,1,512]{2,1,0:T(1,128)}), f32[8,1,512]{2,1,0:T(1,128)S(1)}, u32[]{:S(2)}, u32[]{:S(2)}) async-start(f32[8,1,512]{2,1,0:T(1,128)} %broadcast_in_dim.43), calls=%async_computation.3 | async-start | bytes 32768 | tf_op jit(solution)/shard_map/all_to_all | solution.py:14
  397.5 9.8 %all-to-all-start.6 = ((f32[8,1,64]{2,1,0:T(1,128)}), f32[8,1,64]{2,1,0:T(1,128)S(1)}, u32[]{:S(2)}, u32[]{:S(2)}) async-start(f32[8,1,64]{2,1,0:T(1,128)} %broadcast_in_dim.50), calls=%async_computation.6 | async-start | bytes 8192 | tf_op jit(solution)/shard_map/all_to_all | solution.py:14
  408.0 12.7 %all-to-all-start.4 = ((f32[8,1,1536]{2,1,0:T(1,128)}), f32[8,1,1536]{2,1,0:T(1,128)S(1)}, u32[]{:S(2)}, u32[]{:S(2)}) async-start(f32[8,1,1536]{2,1,0:T(1,128)} %broadcast_in_dim.45), calls=%async_computation.4 | async-start | bytes 98304 | tf_op jit(solution)/shard_map/all_to_all | solution.py:14
  420.7 26.8 %copy-start.1 = (f32[512]{0:T(512)}, f32[512]{0:T(512)S(1)}, u32[]{:S(2)}) copy-start(f32[512]{0:T(512)S(1)} %get-tuple-element.20) | copy-start | bytes 6148
